TPU v7x, 256 devices: a whole 4x4x8 slice. The times are simulated.
256 devices in a mesh: ctx: 16 (over z, core), grp: 16 (over x, y).
Axes of the slice: x: 4, y: 4, z: 8, core: 2. Of those that a mesh axis runs over, the one named last changes fastest.
Arguments:
- queries: bfloat16 [4096, 8192], P('ctx', 'grp'), may hold values from -27 to 27, as said below
- keys: bfloat16 [4096, 1024], P('ctx'), may hold values from -27 to 27
- values: bfloat16 [4096, 1024], P('ctx'), may hold values from -6 to 6
- out_weight: bfloat16 [8192, 8192], P('grp'), may hold values from -0.0625 to 0.0625
- span_order: int32 [32], replicated, may hold values from 0 to 31, each once
- document: int32 [4096], replicated, may hold values from 0 to 3, never falling along the last dimension, each value on 1 to 2048 neighbouring positions
Outputs:
- projected: bfloat16 [4096, 8192], P('ctx', 'grp')
Inputs may be any that keep to these rules, and one draw needn't show every extreme that they name: `queries`: queries and keys are of order one, except a few rows that may be larger.
All inputs are finite; a program needn't handle non-finite values.
Results may differ from a plain program's by a relative error of at most 0.023.
Values may be sent and summed in bfloat16 or wider, within the bound.
A program may use at most 128 MiB of HBM per device.

v0:
```python
import math

import jax
import jax.numpy as jnp
from jax import lax
from jax.sharding import PartitionSpec as P

HEAD_DIM = 128
QUERY_GROUP = 8


def in_one_piece(arrays, axis, dim, along):
    ends, at = ([], 0)
    for a in arrays[:-1]:
        at += a.shape[along]
        ends.append(at)
    both = jnp.concatenate(arrays, axis=along)
    return tuple(jnp.split(lax.all_gather(both, axis, axis=dim, tiled=True), ends, axis=along))


def cut_along(x, dim, count):
    shape = x.shape
    parts = x.reshape(*shape[:dim], count, shape[dim] // count, *shape[dim + 1 :])
    return jnp.moveaxis(parts, dim, 0)


def summed_on_arrival(x, axis, dim):
    parts = cut_along(x, dim, lax.axis_size(axis))
    arrived = lax.all_to_all(parts, axis, split_axis=0, concat_axis=0, tiled=True)
    return arrived.astype(jnp.float32).sum(axis=0)


def span_positions(span_order, first_row, count, tok_rows):
    rows = first_row + jnp.arange(count, dtype=jnp.int32)
    span_len = tok_rows // 2
    return jnp.take(span_order, rows // span_len) * span_len + rows % span_len


def attend(
    state, query_block, query_pos, query_doc, key_block, value_block, key_pos, key_doc, kv_heads
):
    out_acc, run_max, run_sum = state
    rows = query_block.shape[0]
    count = key_block.shape[0]
    group_size = query_block.shape[1] // (kv_heads * HEAD_DIM)
    grouped = query_block.reshape(rows, kv_heads, group_size, HEAD_DIM)
    key_view = key_block.reshape(count, kv_heads, HEAD_DIM)
    value_view = value_block.reshape(count, kv_heads, HEAD_DIM)
    scores = jnp.einsum("rkgd,skd->kgrs", grouped, key_view, preferred_element_type=jnp.float32)
    scores = scores * (1.0 / math.sqrt(HEAD_DIM))
    visible = (key_pos[None, :] <= query_pos[:, None]) & (key_doc[None, :] == query_doc[:, None])
    scores = jnp.where(visible, scores, -jnp.inf)
    new_max = jnp.max(scores, axis=-1)
    safe_max = jnp.where(new_max == -jnp.inf, 0.0, new_max)
    rescale = jnp.exp(run_max - safe_max)
    probs = jnp.exp(scores - safe_max[..., None])
    new_sum = run_sum * rescale + jnp.sum(probs, axis=-1)
    mixed = jnp.einsum(
        "kgrs,skd->kgrd", probs.astype(jnp.bfloat16), value_view, preferred_element_type=jnp.float32
    )
    return (out_acc * rescale[..., None] + mixed, new_max, new_sum)


def shards(queries, keys, values, out_weight, span_order, document):
    own_index = lax.axis_index("ctx")
    group_index = lax.axis_index("grp")
    tok_rows = queries.shape[0]
    local_heads = queries.shape[1] // HEAD_DIM
    kv_heads = max(1, local_heads // QUERY_GROUP)
    group_size = local_heads // kv_heads
    kv_first = group_index * local_heads // QUERY_GROUP
    key_local = lax.dynamic_slice_in_dim(keys, kv_first * HEAD_DIM, kv_heads * HEAD_DIM, 1)
    value_local = lax.dynamic_slice_in_dim(values, kv_first * HEAD_DIM, kv_heads * HEAD_DIM, 1)
    found = span_positions(span_order, own_index * tok_rows + 0, tok_rows, tok_rows)
    own_doc = jnp.take(document, found)
    start_state = (
        jnp.zeros((kv_heads, group_size, tok_rows, HEAD_DIM), jnp.float32),
        jnp.full((kv_heads, group_size, tok_rows), -jnp.inf, jnp.float32),
        jnp.zeros((kv_heads, group_size, tok_rows), jnp.float32),
    )
    pieces = in_one_piece((key_local, value_local), "ctx", 0, 1)
    count = pieces[0].shape[0]
    key_pos = span_positions(span_order, jnp.int32(0), count, tok_rows)
    key_doc = jnp.take(document, key_pos)
    state = attend(
        start_state, queries, found, own_doc, pieces[0], pieces[1], key_pos, key_doc, kv_heads
    )
    out_acc, run_max, run_sum = state
    attended = (out_acc / run_sum[..., None]).astype(jnp.bfloat16)
    weight_view = out_weight.reshape(kv_heads, group_size, HEAD_DIM, out_weight.shape[1])
    partial_value = jnp.einsum(
        "kgrd,kgdm->rm", attended, weight_view, preferred_element_type=jnp.float32
    )
    return summed_on_arrival(partial_value.astype(jnp.bfloat16), "grp", 1).astype(jnp.bfloat16)


def solution(mesh):
    in_specs = (P("ctx", "grp"), P("ctx", None), P("ctx", None), P("grp", None), P(), P())
    out_specs = P("ctx", "grp")
    return jax.shard_map(shards, mesh=mesh, in_specs=in_specs, out_specs=out_specs, check_vma=False)
```

profile of v0, /device:TPU:32, one launch (start us, length us, event | category | flops | bytes accessed | tf_op | source)
XLA Modules:
  0.0 175.0 jit_solution(3079316423473608644)
XLA Ops:
  6.5 0.9 constant_dynamic-slice_fusion
  7.5 0.7 pad_maximum_fusion
  8.6 1.8 %fusion.47 = (s32[1]{0:T(128)}, s32[1]{0:T(128)}, s32[1]{0:T(128)}, s32[1]{0:T(128)}, s32[1]{0:T(128)}, /*index=5*/s32[1]{0:T(128)}, s32[1]{0:T(128)}, s32[1]{0:...) fusion(s32[32]{0:T(128)} %param.10), kind=kLoop, calls=%fused_computation.147 | loop fusion | bytes 104 | tf_op jit(solution)/shard_map/jit(_take)/gather | solution.py:36
  10.4 2.1 %fusion.46 = (s32[1]{0:T(128)}, s32[1]{0:T(128)}, s32[1]{0:T(128)}, s32[1]{0:T(128)}, s32[1]{0:T(128)}, /*index=5*/s32[1]{0:T(128)}, s32[1]{0:T(128)}, s32[1]{0:...) fusion(s32[32]{0:T(128)} %param.10), kind=kLoop, calls=%fused_computation.146 | loop fusion | bytes 152 | tf_op jit(solution)/shard_map/jit(_take)/gather | solution.py:36
  12.5 4.4 %compare_select_fusion.13 = s32[256,1]{0,1:T(1,128)S(1)} fusion(s32[]{:T(128)} %bitcast.25, s32[]{:T(128)} %bitcast.26, s32[]{:T(128)} %bitcast.27, s32[]{:T(128)} %bitcast.28, s32[]{:T(128)} %bitcast.29, s32[]{:T(128)} %bitcast.31, s32[]{:T(128)} %bitcast.30, s32[]{:T(128)S(6)} %mul.71), kind=kLoop, calls=%fused_computation.115 | loop fusion | flops 7936 | bytes 1056 | tf_op jit(solution)/shard_map/jit(_take)/gather | solution.py:36
  16.9 15.7 %select_select_fusion.1 = s32[256]{0:T(256)S(1)} fusion(pred[256]{0:T(512)(128)(4,1)S(1)} %get-tuple-element.47, pred[256]{0:T(512)(128)(4,1)S(1)} %get-tuple-element.48, pred[256]{0:T(512)(128)(4,1)S(1)} %get-tuple-element.49, pred[256]{0:T(512)(128)(4,1)S(1)} %get-tuple-element.50, pred[256]{0:T(512)(128)(4,1)S(1)} %get-tuple-element.51, ...), kind=kLoop, calls=%fused_computation.139 | loop fusion | flops 6400 | bytes 8548 | tf_op jit(solution)/shard_map/jit(_take)/gather | solution.py:36
  32.6 2.0 %gather_fusion.1 = s32[256]{0:T(256)S(1)} fusion(s32[4096]{0:T(1024)} %param.11, s32[1024]{0:T(1024)S(1)} %pad_clamp_fusion), kind=kCustom, calls=%fused_computation.1 | custom fusion | bytes 3072 | tf_op jit(solution)/shard_map/jit(_take)/gather | solution.py:75
  34.6 0.1 compare_reduce_fusion.23
  34.7 0.1 compare_reduce_fusion.22
  34.8 0.1 compare_reduce_fusion.20
  34.9 0.1 compare_reduce_fusion.18
  35.0 0.1 compare_reduce_fusion.16
  35.2 0.1 compare_reduce_fusion.14
  36.0 4.3 %compare_select_fusion.2 = s32[4096,1]{0,1:T(1,128)S(1)} fusion(s32[]{:T(128)} %bitcast.25, s32[]{:T(128)} %bitcast.26, s32[]{:T(128)} %bitcast.27, s32[]{:T(128)} %bitcast.28, s32[]{:T(128)} %bitcast.29, s32[]{:T(128)} %bitcast.31, s32[]{:T(128)} %bitcast.30), kind=kLoop, calls=%fused_computation.52 | loop fusion | flops 94208 | bytes 16412 | tf_op jit(solution)/shard_map/jit(_take)/gather | solution.py:36
  40.4 15.8 %select_select_fusion = s32[4096]{0:T(1024)S(1)} fusion(pred[4096]{0:T(1024)(128)(4,1)S(1)} %compare_reduce_fusion, pred[4096]{0:T(1024)(128)(4,1)S(1)} %compare_reduce_fusion.1, pred[4096]{0:T(1024)(128)(4,1)S(1)} %compare_reduce_fusion.2, pred[4096]{0:T(1024)(128)(4,1)S(1)} %compare_reduce_fusion.3, pred[4096]{0:T(1024)(128)(4,1)S(1)} %compare_reduce_fusion.4, ...), kind=kLoop, calls=%fused_computation.81 | loop fusion | flops 102400 | bytes 135268 | tf_op jit(solution)/shard_map/jit(_take)/gather | solution.py:36
  56.2 19.3 %gather_fusion = s32[4096]{0:T(1024)S(1)} fusion(s32[4096]{0:T(1024)} %param.11, s32[4096]{0:T(1024)S(1)} %broadcast_clamp_fusion), kind=kCustom, calls=%fused_computation | custom fusion | bytes 49152 | tf_op jit(solution)/shard_map/jit(_take)/gather | solution.py:84
  75.5 1.4 compare_and_fusion
  77.0 4.0 %fusion.2 = (f32[4,256]{1,0:T(4,128)S(1)}, f32[4096,256,4]{1,0,2:T(8,128)S(1)}) fusion(pred[256,4096]{0,1:T(8,128)(4,1)S(1)} %compare_and_fusion, bf16[4096,256]{1,0:T(8,128)(2,1)} %all-gather.2.cloned.1.call-done, bf16[256,512]{1,0:T(8,128)(2,1)S(1)} %copy-done), kind=kOutput, calls=%fused_computation.6 | convolution fusion | flops 1086323712 | bytes 19140608 | tf_op jit(solution)/shard_map/rkgd,skd->kgrs/dot_general | solution.py:49
  81.0 5.7 %copy-done.1 = f32[4096,256,4]{1,0,2:T(8,128)} copy-done((f32[4096,256,4]{1,0,2:T(8,128)}, f32[4096,256,4]{1,0,2:T(8,128)S(1)}, u32[]{:S(2)}) %copy-start.1) | copy-done | bytes 16777240
  86.7 3.6 %fusion = f32[4,256]{1,0:T(4,128)S(1)} fusion(f32[4096,256,4]{1,0,2:T(8,128)S(1)} %get-tuple-element.44, f32[4,256]{1,0:T(4,128)S(1)} %compare_select_fusion.10, pred[256,4096]{0,1:T(8,128)(4,1)S(1)} %compare_and_fusion), kind=kLoop, calls=%fused_computation.4 | loop fusion | flops 16776192 | bytes 17833984 | tf_op jit(solution)/shard_map/reduce_sum | solution.py:57
  90.4 13.9 %fusion.3 = bf16[256,8192]{1,0:T(8,128)(2,1)} fusion(bf16[4,128,8192]{2,1,0:T(8,128)(2,1)} %bitcast.114, bf16[4096,256]{1,0:T(8,128)(2,1)S(1)} %copy-done.2, f32[4096,256,4]{1,0,2:T(8,128)} %copy-done.1, f32[4,256]{1,0:T(4,128)S(1)} %compare_select_fusion.10, pred[256,4096]{0,1:T(8,128)(4,1)S(1)} %compare_and_fusion, f32[4,256]{1,0:T(4,128)S(1)} %get-tuple-element.10, ...), kind=kOutput, calls=%fused_computation.8 | convolution fusion | flops 3240493056 | bytes 31469568 | tf_op jit(solution)/shard_map/kgrd,kgdm->rm/dot_general | solution.py:91
  104.3 2.6 %copy.22 = bf16[32,16,8,512]{3,2,0,1:T(8,128)(2,1)S(1)} copy(bf16[32,16,8,512]{3,2,1,0:T(8,128)(2,1)} %bitcast.107) | data formatting | bytes 8388608 | tf_op jit(solution)/shard_map/reshape | solution.py:23
  106.9 57.7 %all_to_all.5 = bf16[16,256,512]{2,1,0:T(8,128)(2,1)} all-to-all(bf16[16,256,512]{2,1,0:T(8,128)(2,1)S(1)} %bitcast.106), channel_id=1, replica_groups=mesh['ctx'=16,'grp'=16] {'grp'}, dimensions={0} | all-to-all | bytes 8388608 | tf_op jit(solution)/shard_map/all_to_all | solution.py:29
  164.6 3.5 %reduce_sum.22 = bf16[256,512]{1,0:T(8,128)(2,1)} reduce(bf16[16,256,512]{2,1,0:T(8,128)(2,1)} %all_to_all.5, bf16[]{:T(256)} %constant.148.clone.1), dimensions={0}, to_apply=%region_2.3 | reduce | flops 1966080 | bytes 4456450 | tf_op jit(solution)/shard_map/reduce_sum | solution.py:30
  (48 shorter events, 1.7 us)
Async XLA Ops:
  6.5 70.5 %copy-start = (bf16[256,512]{1,0:T(8,128)(2,1)S(1)}, bf16[256,512]{1,0:T(8,128)(2,1)}, u32[]{:S(2)}) copy-start(bf16[256,512]{1,0:T(8,128)(2,1)} %param.6) | copy-start | bytes 786436
  6.5 70.4 %all-gather.2.cloned.1.call-start = ((), (), s32[]{:S(2)}) async-start(), calls=%async_computation.1 | async-start | bytes 2228224 | tf_op jit(solution)/shard_map/all_gather | solution.py:18
  77.0 13.4 %copy-start.2 = (bf16[4096,256]{1,0:T(8,128)(2,1)S(1)}, bf16[4096,256]{1,0:T(8,128)(2,1)}, u32[]{:S(2)}) copy-start(bf16[4096,256]{1,0:T(8,128)(2,1)} %all-gather.2.cloned.1.call-done) | copy-start | bytes 6291460
  81.0 5.7 %copy-start.1 = (f32[4096,256,4]{1,0,2:T(8,128)}, f32[4096,256,4]{1,0,2:T(8,128)S(1)}, u32[]{:S(2)}) copy-start(f32[4096,256,4]{1,0,2:T(8,128)S(1)} %get-tuple-element.44) | copy-start | bytes 50331652
Sparse Core Ops, SparseCore 0:
  9.2 41.5 all-gather.1
where the time goes:
time: 176 us; the launch traced here: 175 us
  blocking collectives  57.7 us (33%)
  other arithmetic  51.4 us (29%)
  local copies, waits for them, and re-layouts  34.4 us (20%)
  matrix products  17.9 us (10%)
  between operations  13.6 us (8%)
    all_to_all x1, blocking collectives, summed_on_arrival(): lax.all_to_all(parts, axis, split_axis=0, concat_axis=0, tiled=True)  57.7 us
    gather x42, other arithmetic, span_positions(): return jnp.take(span_order, rows // span_len) * span_len + rows % span_len  42 us
    gather x1, local copies, waits for them, and re-layouts, shards(): key_doc = jnp.take(document, key_pos)  19.3 us
    dot_general x1, matrix products, shards(): jnp.einsum('kgrd,kgdm->rm', attended, weight_view, preferred_element_type...  13.9 us
    unnamed x6, local copies, waits for them, and re-layouts  5.7 us
    dot_general x1, matrix products, attend(): jnp.einsum('rkgd,skd->kgrs', grouped, key_view, preferred_element_type=jn...  4 us
    gather x2, local copies, waits for them, and re-layouts, span_positions(): return jnp.take(span_order, rows // span_len) * span_len + rows % span_len  3.91 us
    reduce_sum x1, other arithmetic, attend(): new_sum = run_sum * rescale + jnp.sum(probs, axis=-1)  3.61 us
  transfers between devices with their start and end apart: 1, of which 0 were waited for; matrix products, arithmetic and copies ran while one was open for 39% of the time, Pallas kernels for 0%

commit v1 on v0

v1 whole, which is shorter than its diff:
```python
import math

import jax
import jax.numpy as jnp
from jax import lax
from jax.experimental import pallas as pl
from jax.experimental.pallas import tpu as pltpu
from jax.sharding import PartitionSpec as P

MESH = pl.DeviceIdType.MESH
F32, BF16 = jnp.float32, jnp.bfloat16
HEAD = 128
SPAN = 128
HEADS = 4
ROWS = 256
SIDE = 4
DEPTH = 8
PER = 512
HALF = PER // 2
NB = 2
RB = ROWS // 2 // NB
LOW = -1e30
TO_LOG2 = math.log2(math.e) / math.sqrt(HEAD)


def wrap(v, n):
    return lax.rem(v + n, n)


def kernel(
    span_ref, doc_ref, q_hbm, k_hbm, v_hbm, w_hbm, out_ref,
    qbuf, kbuf, vbuf, wbuf, acc, top, att, first, send1, recv1, send2, recv2,
    load_sem, z_send, z_recv, s_send, s_recv, send1_sem, recv1_sem, send2_sem, recv2_sem,
):
    ctx, grp = lax.axis_index("ctx"), lax.axis_index("grp")
    z, core = lax.div(ctx, 2), lax.rem(ctx, 2)
    x, y = lax.div(grp, SIDE), lax.rem(grp, SIDE)
    other = 2 * z + 1 - core
    z_next = [{"ctx": 2 * wrap(z + s, DEPTH) + core} for s in (1, -1)]
    x_next = [{"grp": wrap(x + s, SIDE) * SIDE + y} for s in (1, -1)]
    y_next = [{"grp": x * SIDE + wrap(y + s, SIDE)} for s in (1, -1)]
    sibling = {"ctx": other}

    barrier = pltpu.get_barrier_semaphore()
    for there in z_next + x_next + y_next + [sibling]:
        pl.semaphore_signal(barrier, inc=1, device_id=there, device_id_type=MESH)

    head_cols = pl.ds(pl.multiple_of(lax.div(grp, 2) * HEAD, HEAD), HEAD)
    load_k = pltpu.make_async_copy(k_hbm.at[:, head_cols], kbuf.at[ctx], load_sem.at[0])
    load_v = pltpu.make_async_copy(v_hbm.at[:, head_cols], vbuf.at[ctx], load_sem.at[1])
    load_k.start()
    load_v.start()
    load_q = [
        pltpu.make_async_copy(q_hbm.at[:, pl.ds(h * HEAD, HEAD)], qbuf.at[h], load_sem.at[2 + h])
        for h in range(HEADS)
    ]
    for c in load_q:
        c.start()
    load_w = [
        pltpu.make_async_copy(
            w_hbm.at[pl.ds(h * HEAD, HEAD)], wbuf.at[pl.ds(h * HEAD, HEAD)], load_sem.at[6 + h]
        )
        for h in range(HEADS)
    ]
    for c in load_w:
        c.start()

    acc[...] = jnp.zeros_like(acc)
    top[...] = jnp.full(top.shape, LOW, F32)

    def positions(slot, shape, dim):
        return (span_ref[slot] * SPAN + lax.broadcasted_iota(jnp.int32, shape, dim)).astype(F32)

    doc = doc_ref[...]
    starts = []
    for d in range(1, 4):
        before = jnp.sum(jnp.where(doc < d, 1.0, 0.0), axis=0, keepdims=True)
        starts.append(jnp.sum(before, axis=1, keepdims=True))
    for a in range(2):
        at = positions(2 * ctx + a, (SPAN, SPAN), 0)
        begin = jnp.zeros((SPAN, SPAN), F32)
        for s in starts:
            begin = jnp.maximum(begin, jnp.where(at >= s, s, 0.0))
        first[pl.ds(a * SPAN, SPAN), :] = begin

    load_k.wait()
    load_v.wait()
    pl.semaphore_wait(barrier, 7)

    bufs = (kbuf, vbuf)

    def to_sibling(slot, step, kv):
        return pltpu.make_async_remote_copy(
            src_ref=bufs[kv].at[slot], dst_ref=bufs[kv].at[slot],
            send_sem=s_send.at[step, kv], recv_sem=s_recv.at[step, kv],
            device_id=sibling, device_id_type=MESH,
        )

    def along_z(slot, way, step, kv):
        return pltpu.make_async_remote_copy(
            src_ref=bufs[kv].at[slot], dst_ref=bufs[kv].at[slot],
            send_sem=z_send.at[way, step, kv], recv_sem=z_recv.at[way, step, kv],
            device_id=z_next[way], device_id_type=MESH,
        )

    pending = []

    def go(copy):
        copy.start()
        pending.append(copy)

    for kv in range(2):
        for way in range(2):
            go(along_z(ctx, way, 0, kv))
        go(to_sibling(ctx, 0, kv))

    for c in load_q:
        c.wait()

    def attend(zz):
        key_at = jnp.concatenate([positions(4 * zz + i, (1, SPAN), 1) for i in range(4)], axis=1)
        keys = kbuf[pl.ds(2 * zz, 2)].reshape(2 * ROWS, HEAD)
        values = vbuf[pl.ds(2 * zz, 2)].reshape(2 * ROWS, HEAD)
        values = jnp.concatenate([values, jnp.ones_like(values)], axis=1)
        hide = []
        for a in range(2):
            at = positions(2 * ctx + a, (SPAN, 4 * SPAN), 0)
            begin = jnp.concatenate([first[pl.ds(a * SPAN, SPAN), :]] * 4, axis=1)
            seen = (key_at <= at) & (key_at >= begin)
            hide.append(jnp.where(seen, 0.0, LOW))
        hide = jnp.concatenate(hide, axis=0)
        for h in range(HEADS):
            s = lax.dot_general(
                qbuf[h], keys, (((1,), (1,)), ((), ())), preferred_element_type=F32
            )
            s = s * TO_LOG2 + hide
            old = top[h]
            new = jnp.maximum(old, jnp.max(s, axis=1, keepdims=True))
            probs = jnp.exp2(s - jnp.concatenate([new] * 4, axis=1)).astype(BF16)
            shrink = jnp.exp2(old - new)
            top[h] = new
            acc[h] = acc[h] * jnp.concatenate([shrink] * 2, axis=1) + jnp.dot(
                probs, values, preferred_element_type=F32
            )

    def slot_of(way, step):
        return 2 * wrap(z + (-step if way == 0 else step), DEPTH) + core

    for step in range(1, 5):
        for kv in range(2):
            for way in range(2):
                if step == 4 and kv != way:
                    continue
                slot = slot_of(way, step)
                along_z(slot, way, step - 1, kv).wait_recv()
                if step < 3 or (step == 3 and kv == way):
                    go(along_z(slot, way, step, kv))
                go(to_sibling(slot, step if way == 0 else step + 3, kv) if step < 4
                   else to_sibling(slot, 7, kv))
        if step == 1:
            for kv in range(2):
                to_sibling(other, 0, kv).wait_recv()
            attend(z)
        else:
            for way in range(2):
                for kv in range(2):
                    to_sibling(other, step - 1 if way == 0 else step + 2, kv).wait_recv()
                attend(wrap(z + (1 - step if way == 0 else step - 1), DEPTH))
    for kv in range(2):
        to_sibling(other, 7, kv).wait_recv()
    attend(wrap(z + 4, DEPTH))

    for h in range(HEADS):
        whole = acc[h]
        att[:, pl.ds(h * HEAD, HEAD)] = (whole[:, :HEAD] / whole[:, HEAD:]).astype(BF16)
    for c in load_w:
        c.wait()

    mine = ((x, y), (y, x))
    nexts = ((x_next, y_next), (y_next, x_next))

    def own(half, a, b, row):
        target = a * SIDE + b if half == 0 else b * SIDE + a
        col = pl.multiple_of(target * PER + half * HALF, HALF)
        return jnp.dot(
            att[pl.ds(row, RB), :], wbuf[:, pl.ds(col, HALF)], preferred_element_type=F32
        )

    def row_of(side, batch):
        return side * (ROWS // 2) + batch * RB

    def side_of(way, kind):
        return 1 - way if kind == 1 else way

    def copy1(half, batch, way, kind):
        at = ((half * NB + batch) * 2 + way) * 3 + kind
        return pltpu.make_async_remote_copy(
            src_ref=send1.at[at], dst_ref=recv1.at[at],
            send_sem=send1_sem.at[at], recv_sem=recv1_sem.at[at],
            device_id=nexts[half][0][way], device_id_type=MESH,
        )

    def copy2(half, batch, way, kind):
        at = ((half * NB + batch) * 2 + way) * 3 + kind
        return pltpu.make_async_remote_copy(
            src_ref=send2.at[at], dst_ref=recv2.at[at],
            send_sem=send2_sem.at[at], recv_sem=recv2_sem.at[at],
            device_id=nexts[half][1][way], device_id_type=MESH,
        )

    def index(half, batch, way, kind):
        return ((half * NB + batch) * 2 + way) * 3 + kind

    def stage1(half, batch, way, kind):
        at = index(half, batch, way, kind)
        row = row_of(side_of(way, kind), batch)
        far = 2 if kind == 0 else 1
        a = wrap(mine[half][0] + (far if way == 0 else -far), SIDE)
        if kind == 2:
            copy1(half, batch, way, 0).wait_recv()

        def part(b, carry):
            cols = pl.ds(pl.multiple_of(b * HALF, HALF), HALF)
            value = own(half, a, b, row)
            if kind == 2:
                value = value + recv1[index(half, batch, way, 0), :, cols].astype(F32)
            send1[at, :, cols] = value.astype(BF16)
            return carry

        lax.fori_loop(0, SIDE, part, 0)
        go(copy1(half, batch, way, kind))

    def arrived1(half, batch):
        for way in range(2):
            for kind in (1, 2):
                copy1(half, batch, way, kind).wait_recv()

    def sum1(half, batch, b, side):
        value = own(half, mine[half][0], b, row_of(side, batch))
        cols = pl.ds(pl.multiple_of(b * HALF, HALF), HALF)
        for way in range(2):
            kind = 2 if way == side else 1
            value = value + recv1[index(half, batch, way, kind), :, cols].astype(F32)
        return value

    def stage2(half, batch, way, kind):
        at = index(half, batch, way, kind)
        far = 2 if kind == 0 else 1
        b = wrap(mine[half][1] + (far if way == 0 else -far), SIDE)
        value = sum1(half, batch, b, side_of(way, kind))
        if kind == 2:
            copy2(half, batch, way, 0).wait_recv()
            value = value + recv2[index(half, batch, way, 0)].astype(F32)
        send2[at] = value.astype(BF16)
        go(copy2(half, batch, way, kind))

    def finish(half, batch):
        for side in range(2):
            value = sum1(half, batch, mine[half][1], side)
            for way in range(2):
                kind = 2 if way == side else 1
                copy2(half, batch, way, kind).wait_recv()
                value = value + recv2[index(half, batch, way, kind)].astype(F32)
            out_ref[pl.ds(row_of(side, batch), RB), pl.ds(half * HALF, HALF)] = value.astype(BF16)

    def each(step, batch, kind):
        for way in range(2):
            for half in range(2):
                step(half, batch, way, kind)

    for batch in range(NB):
        each(stage1, batch, 0)
        each(stage1, batch, 1)
        if batch > 0:
            for half in range(2):
                arrived1(half, batch - 1)
            each(stage2, batch - 1, 0)
            each(stage2, batch - 1, 1)
        each(stage1, batch, 2)
        if batch > 0:
            each(stage2, batch - 1, 2)
    for half in range(2):
        arrived1(half, NB - 1)
    each(stage2, NB - 1, 0)
    each(stage2, NB - 1, 1)
    for batch in range(NB - 1):
        for half in range(2):
            finish(half, batch)
    each(stage2, NB - 1, 2)
    for half in range(2):
        finish(half, NB - 1)
    for copy in pending:
        copy.wait_send()


def shards(queries, keys, values, out_weight, span_order, document):
    count = 2 * NB * 2 * 3
    anywhere = pl.BlockSpec(memory_space=pl.ANY)
    in_vmem = pl.BlockSpec(memory_space=pltpu.VMEM)
    dma = pltpu.SemaphoreType.DMA
    return pl.pallas_call(
        kernel,
        out_shape=jax.ShapeDtypeStruct((ROWS, PER), BF16),
        in_specs=[pl.BlockSpec(memory_space=pltpu.SMEM), in_vmem] + [anywhere] * 4,
        out_specs=in_vmem,
        scratch_shapes=[
            pltpu.VMEM((HEADS, ROWS, HEAD), BF16),
            pltpu.VMEM((2 * DEPTH, ROWS, HEAD), BF16),
            pltpu.VMEM((2 * DEPTH, ROWS, HEAD), BF16),
            pltpu.VMEM((HEADS * HEAD, SIDE * SIDE * PER), BF16),
            pltpu.VMEM((HEADS, ROWS, 2 * HEAD), F32),
            pltpu.VMEM((HEADS, ROWS, HEAD), F32),
            pltpu.VMEM((ROWS, HEADS * HEAD), BF16),
            pltpu.VMEM((ROWS, HEAD), F32),
            pltpu.VMEM((count, RB, SIDE * HALF), BF16),
            pltpu.VMEM((count, RB, SIDE * HALF), BF16),
            pltpu.VMEM((count, RB, HALF), BF16),
            pltpu.VMEM((count, RB, HALF), BF16),
            dma((10,)),
            dma((2, 4, 2)),
            dma((2, 4, 2)),
            dma((8, 2)),
            dma((8, 2)),
            dma((count,)),
            dma((count,)),
            dma((count,)),
            dma((count,)),
        ],
        compiler_params=pltpu.CompilerParams(
            collective_id=0, has_side_effects=True, vmem_limit_bytes=60 * 1024 * 1024
        ),
        name="attend_project",
    )(span_order, document.reshape(32, 128), queries, keys, values, out_weight)


def solution(mesh):
    in_specs = (P("ctx", "grp"), P("ctx", None), P("ctx", None), P("grp", None), P(), P())
    return jax.shard_map(
        shards, mesh=mesh, in_specs=in_specs, out_specs=P("ctx", "grp"), check_vma=False
    )
```

time: 176 us -> 63.7 us (0.36)
  Pallas kernels: 0 us -> 61.9 us
  blocking collectives: 57.7 us -> 0 us
  other arithmetic: 51.4 us -> 0 us
  local copies, waits for them, and re-layouts: 34.4 us -> 1.67 us
  matrix products: 17.9 us -> 0 us
  between operations: 13.6 us -> 0.01 us
    pallas_call x0 -> x1, Pallas kernels: none -> 61.9 us  [shards(): pl.pallas_call(kernel, out_shape=jax.ShapeDtypeStruct((ROWS, PER), BF16),...]
    all_to_all x1 -> x0, blocking collectives: 57.7 us -> none  [summed_on_arrival(): lax.all_to_all(parts, axis, split_axis=0, concat_axis=0, tiled=True)]
    gather x44 -> x0, other arithmetic: 42 us -> none  [the longest x42 42 us: span_positions(): return jnp.take(span_order, rows // span_len) * span_len + rows % span_len]
    gather x4 -> x0, local copies, waits for them, and re-layouts: 25.2 us -> none  [the longest x1 19.3 us: shards(): key_doc = jnp.take(document, key_pos)]
    dot_general x2 -> x0, matrix products: 17.9 us -> none  [the longest x1 13.9 us: shards(): jnp.einsum('kgrd,kgdm->rm', attended, weight_view, preferred_element_type...]
    reduce_sum x2 -> x0, other arithmetic: 7.16 us -> none  [the longest x1 3.61 us: attend(): new_sum = run_sum * rescale + jnp.sum(probs, axis=-1)]
    unnamed x6 -> x1, local copies, waits for them, and re-layouts: 5.7 us -> 1.67 us
    reshape x1 -> x0, local copies, waits for them, and re-layouts: 2.63 us -> none  [cut_along(): x.reshape(*shape[:dim], count, shape[dim] // count, *shape[dim + 1:])]
  transfers between devices with their start and end apart: 1 -> 0, of which waited for: 0 -> 0; matrix products, arithmetic and copies ran while one was open for 39% -> 0% of each run, Pallas kernels for 0% -> 0%
where the time goes in v1:
time: 63.7 us; the launch traced here: 63.5 us
  Pallas kernels  61.9 us (97%)
  local copies, waits for them, and re-layouts  1.67 us (3%)
    pallas_call x1, Pallas kernels, shards(): pl.pallas_call(kernel, out_shape=jax.ShapeDtypeStruct((ROWS, PER), BF16),...  61.9 us
    unnamed x1, local copies, waits for them, and re-layouts  1.67 us

profile of v1, /device:TPU:32, one launch (start us, length us, event | category | flops | bytes accessed | tf_op | source)
XLA Modules:
  0.0 63.5 jit_solution(6042484448733477492)
XLA Ops:
  0.0 61.9 %attend_project.1 = bf16[256,512]{1,0:T(8,128)(2,1)} custom-call(s32[32]{0:T(128)} %span_ref.1, s32[32,128]{1,0:T(8,128)} %bitcast.1, bf16[256,512]{1,0:T(8,128)(2,1)} %q_hbm.1, bf16[256,1024]{1,0:T(8,128)(2,1)} %k_hbm.1, bf16[256,1024]{1,0:T(8,128)(2,1)} %v_hbm.1, bf16[512,8192]{1,0:T(8,128)(2,1)} %w_hbm.1), custom_call_target="tpu_custom_call" | custom-call | tf_op jit(solution)/shard_map/attend_project/pallas_call | solution.py:301
  61.9 1.7 %copy.8 = bf16[256,512]{1,0:T(8,128)(2,1)} copy(bf16[256,512]{1,0:T(8,128)(2,1)} %attend_project.1) | data formatting | bytes 524288

commit v2 on v1

v2 whole, which is shorter than its diff:
```python
import math

import jax
import jax.numpy as jnp
from jax import lax
from jax.experimental import pallas as pl
from jax.experimental.pallas import tpu as pltpu
from jax.sharding import PartitionSpec as P

MESH = pl.DeviceIdType.MESH
F32, BF16 = jnp.float32, jnp.bfloat16
HEAD = 128
SPAN = 128
HEADS = 4
ROWS = 256
SIDE = 4
DEPTH = 8
PER = 512
HALF = PER // 2
SIDES = ROWS // 2
LOW = -1e30
TO_LOG2 = math.log2(math.e) / math.sqrt(HEAD)


def wrap(v, n):
    return lax.rem(v + n, n)


def kernel(
    span_ref, doc_ref, q_hbm, k_hbm, v_hbm, w_hbm, out_ref,
    qbuf, kbuf, vbuf, wbuf, acc, top, att, hide, send1, recv1, send2, recv2,
    load_sem, z_send, z_recv, s_send, s_recv, send1_sem, recv1_sem, send2_sem, recv2_sem,
):
    ctx, grp = lax.axis_index("ctx"), lax.axis_index("grp")
    z, core = lax.div(ctx, 2), lax.rem(ctx, 2)
    x, y = lax.div(grp, SIDE), lax.rem(grp, SIDE)
    other = 2 * z + 1 - core
    z_next = [{"ctx": 2 * wrap(z + s, DEPTH) + core} for s in (1, -1)]
    x_next = [{"grp": wrap(x + s, SIDE) * SIDE + y} for s in (1, -1)]
    y_next = [{"grp": x * SIDE + wrap(y + s, SIDE)} for s in (1, -1)]
    sibling = {"ctx": other}

    barrier = pltpu.get_barrier_semaphore()
    for there in z_next + x_next + y_next + [sibling]:
        pl.semaphore_signal(barrier, inc=1, device_id=there, device_id_type=MESH)

    head_cols = pl.ds(pl.multiple_of(lax.div(grp, 2) * HEAD, HEAD), HEAD)
    load_k = pltpu.make_async_copy(k_hbm.at[:, head_cols], kbuf.at[ctx], load_sem.at[0])
    load_v = pltpu.make_async_copy(v_hbm.at[:, head_cols], vbuf.at[ctx], load_sem.at[1])
    load_k.start()
    load_v.start()
    load_q = [
        pltpu.make_async_copy(q_hbm.at[:, pl.ds(h * HEAD, HEAD)], qbuf.at[h], load_sem.at[2 + h])
        for h in range(HEADS)
    ]
    for c in load_q:
        c.start()
    load_w = [
        pltpu.make_async_copy(
            w_hbm.at[pl.ds(h * HEAD, HEAD)], wbuf.at[pl.ds(h * HEAD, HEAD)], load_sem.at[6 + h]
        )
        for h in range(HEADS)
    ]
    for c in load_w:
        c.start()

    bufs = (kbuf, vbuf)

    def piece(slot, p):
        return bufs[p // 2].at[slot, pl.ds(p % 2 * SPAN, SPAN)]

    def to_sibling(slot, step, p):
        return pltpu.make_async_remote_copy(
            src_ref=piece(slot, p), dst_ref=piece(slot, p),
            send_sem=s_send.at[step, p], recv_sem=s_recv.at[step, p],
            device_id=sibling, device_id_type=MESH,
        )

    def along_z(slot, way, step, p):
        return pltpu.make_async_remote_copy(
            src_ref=piece(slot, p), dst_ref=piece(slot, p),
            send_sem=z_send.at[way, step, p], recv_sem=z_recv.at[way, step, p],
            device_id=z_next[way], device_id_type=MESH,
        )

    pending = []

    def go(copy):
        copy.start()
        pending.append(copy)

    load_k.wait()
    load_v.wait()
    pl.semaphore_wait(barrier, 7)
    for p in range(4):
        for way in range(2):
            go(along_z(ctx, way, 0, p))
    for p in range(4):
        go(to_sibling(ctx, 0, p))

    acc[...] = jnp.zeros_like(acc)
    top[...] = jnp.full(top.shape, LOW, F32)

    def positions(slot, shape, dim):
        return (span_ref[slot] * SPAN + lax.broadcasted_iota(jnp.int32, shape, dim)).astype(F32)

    doc = doc_ref[...]
    starts = []
    for d in range(1, 4):
        before = jnp.sum(jnp.where(doc < d, 1.0, 0.0), axis=0, keepdims=True)
        starts.append(jnp.sum(before, axis=1, keepdims=True))
    for a in range(2):
        at = positions(2 * ctx + a, (SPAN, SPAN), 0)
        begin = jnp.zeros((SPAN, SPAN), F32)
        for s in starts:
            begin = jnp.maximum(begin, jnp.where(at >= s, s, 0.0))

        def mask(slot, carry):
            key_at = positions(slot, (SPAN, SPAN), 1)
            seen = (key_at <= at) & (key_at >= begin)
            hide[slot // 4, pl.ds(a * SPAN, SPAN), pl.ds(pl.multiple_of(slot % 4 * SPAN, SPAN), SPAN)] = (
                jnp.where(seen, 0.0, LOW)
            )
            return carry

        lax.fori_loop(0, 4 * DEPTH, mask, 0)

    for c in load_q:
        c.wait()

    def attend(zz, h):
        keys = kbuf[pl.ds(2 * zz, 2)].reshape(2 * ROWS, HEAD)
        values = vbuf[pl.ds(2 * zz, 2)].reshape(2 * ROWS, HEAD)
        values = jnp.concatenate([values, jnp.ones_like(values)], axis=1)
        s = lax.dot_general(qbuf[h], keys, (((1,), (1,)), ((), ())), preferred_element_type=F32)
        s = s * TO_LOG2 + hide[zz]
        old = top[h]
        new = jnp.maximum(old, jnp.max(s, axis=1, keepdims=True))
        probs = jnp.exp2(s - jnp.concatenate([new] * 4, axis=1)).astype(BF16)
        shrink = jnp.exp2(old - new)
        top[h] = new
        acc[h] = acc[h] * jnp.concatenate([shrink] * 2, axis=1) + jnp.dot(
            probs, values, preferred_element_type=F32
        )

    def chip(way, step):
        return wrap(z + (-step if way == 0 else step), DEPTH)

    for step in range(1, 5):
        back = step - 1
        if back == 0:
            ready = [(z, 0)]
        else:
            ready = [(chip(way, back), back + 3 * way) for way in range(2)]
        units = [(zz, h) for h in range(HEADS) for zz, _ in ready]
        pieces = range(4) if step < 4 else range(2)
        for p in pieces:
            for way in range(2):
                q = p if step < 4 else 2 * way + p
                slot = 2 * chip(way, step) + core
                along_z(slot, way, step - 1, q).wait_recv()
                if step < 3 or (step == 3 and q // 2 == way):
                    go(along_z(slot, way, step, q))
                go(to_sibling(slot, step + 3 * way if step < 4 else 7, q))
            if p == 0:
                for _, number in ready:
                    for r in range(4):
                        to_sibling(other, number, r).wait_recv()
            share = len(units) // len(pieces)
            for zz, h in units[p * share : (p + 1) * share]:
                attend(zz, h)
    for r in range(4):
        to_sibling(other, 7, r).wait_recv()
    for h in range(HEADS):
        attend(chip(0, 4), h)

    for h in range(HEADS):
        whole = acc[h]
        att[:, pl.ds(h * HEAD, HEAD)] = (whole[:, :HEAD] / whole[:, HEAD:]).astype(BF16)
    for c in load_w:
        c.wait()

    mine = ((x, y), (y, x))
    nexts = ((x_next, y_next), (y_next, x_next))
    offsets = (2, 1, -1, 0)

    def own(half, a, j, side):
        b = wrap(mine[half][1] + offsets[j], SIDE)
        target = a * SIDE + b if half == 0 else b * SIDE + a
        col = pl.multiple_of(target * PER + half * HALF, HALF)
        return jnp.dot(
            att[pl.ds(side * SIDES, SIDES), :], wbuf[:, pl.ds(col, HALF)],
            preferred_element_type=F32,
        )

    def side_of(way, kind):
        return 1 - way if kind == 1 else way

    def at1(half, way, kind, j):
        return ((half * 2 + way) * 3 + kind) * 4 + j

    def at2(half, way, kind):
        return (half * 2 + way) * 3 + kind

    def copy1(half, way, kind, j):
        at = at1(half, way, kind, j)
        return pltpu.make_async_remote_copy(
            src_ref=send1.at[at], dst_ref=recv1.at[at],
            send_sem=send1_sem.at[at], recv_sem=recv1_sem.at[at],
            device_id=nexts[half][0][way], device_id_type=MESH,
        )

    def copy2(half, way, kind):
        at = at2(half, way, kind)
        return pltpu.make_async_remote_copy(
            src_ref=send2.at[at], dst_ref=recv2.at[at],
            send_sem=send2_sem.at[at], recv_sem=recv2_sem.at[at],
            device_id=nexts[half][1][way], device_id_type=MESH,
        )

    def stage1(half, way, kind, j):
        far = 2 if kind == 0 else 1
        a = wrap(mine[half][0] + (far if way == 0 else -far), SIDE)
        value = own(half, a, j, side_of(way, kind))
        if kind == 2:
            copy1(half, way, 0, j).wait_recv()
            value = value + recv1[at1(half, way, 0, j)].astype(F32)
        send1[at1(half, way, kind, j)] = value.astype(BF16)
        go(copy1(half, way, kind, j))

    def arrived1(half, j):
        for way in range(2):
            for kind in (1, 2):
                copy1(half, way, kind, j).wait_recv()

    def sum1(half, j, side):
        value = own(half, mine[half][0], j, side)
        for way in range(2):
            value = value + recv1[at1(half, way, 2 if way == side else 1, j)].astype(F32)
        return value

    def stage2(half, way, kind):
        value = sum1(half, 0 if kind == 0 else 1 + way, side_of(way, kind))
        if kind == 2:
            copy2(half, way, 0).wait_recv()
            value = value + recv2[at2(half, way, 0)].astype(F32)
        send2[at2(half, way, kind)] = value.astype(BF16)
        go(copy2(half, way, kind))

    def each(step, *rest):
        for way in range(2):
            for half in range(2):
                step(half, way, *rest)

    for kind in range(3):
        for j in range(4):
            each(stage1, kind, j)
    for half in range(2):
        arrived1(half, 0)
    each(stage2, 0)
    for j in (1, 2):
        for half in range(2):
            arrived1(half, j)
            stage2(half, j - 1, 1)
    each(stage2, 2)
    for half in range(2):
        arrived1(half, 3)
    for half in range(2):
        for side in range(2):
            value = sum1(half, 3, side)
            for way in range(2):
                kind = 2 if way == side else 1
                copy2(half, way, kind).wait_recv()
                value = value + recv2[at2(half, way, kind)].astype(F32)
            out_ref[pl.ds(side * SIDES, SIDES), pl.ds(half * HALF, HALF)] = value.astype(BF16)
    for copy in pending:
        copy.wait_send()


def shards(queries, keys, values, out_weight, span_order, document):
    anywhere = pl.BlockSpec(memory_space=pl.ANY)
    in_vmem = pl.BlockSpec(memory_space=pltpu.VMEM)
    dma = pltpu.SemaphoreType.DMA
    return pl.pallas_call(
        kernel,
        out_shape=jax.ShapeDtypeStruct((ROWS, PER), BF16),
        in_specs=[pl.BlockSpec(memory_space=pltpu.SMEM), in_vmem] + [anywhere] * 4,
        out_specs=in_vmem,
        scratch_shapes=[
            pltpu.VMEM((HEADS, ROWS, HEAD), BF16),
            pltpu.VMEM((2 * DEPTH, ROWS, HEAD), BF16),
            pltpu.VMEM((2 * DEPTH, ROWS, HEAD), BF16),
            pltpu.VMEM((HEADS * HEAD, SIDE * SIDE * PER), BF16),
            pltpu.VMEM((HEADS, ROWS, 2 * HEAD), F32),
            pltpu.VMEM((HEADS, ROWS, HEAD), F32),
            pltpu.VMEM((ROWS, HEADS * HEAD), BF16),
            pltpu.VMEM((DEPTH, ROWS, 4 * SPAN), F32),
            pltpu.VMEM((48, SIDES, HALF), BF16),
            pltpu.VMEM((48, SIDES, HALF), BF16),
            pltpu.VMEM((12, SIDES, HALF), BF16),
            pltpu.VMEM((12, SIDES, HALF), BF16),
            dma((10,)),
            dma((2, 4, 4)),
            dma((2, 4, 4)),
            dma((8, 4)),
            dma((8, 4)),
            dma((48,)),
            dma((48,)),
            dma((12,)),
            dma((12,)),
        ],
        compiler_params=pltpu.CompilerParams(
            collective_id=0, has_side_effects=True, vmem_limit_bytes=60 * 1024 * 1024
        ),
        name="attend_project",
    )(span_order, document.reshape(32, 128), queries, keys, values, out_weight)


def solution(mesh):
    in_specs = (P("ctx", "grp"), P("ctx", None), P("ctx", None), P("grp", None), P(), P())
    return jax.shard_map(
        shards, mesh=mesh, in_specs=in_specs, out_specs=P("ctx", "grp"), check_vma=False
    )
```

time: 63.7 us -> 57.9 us (0.909)
  Pallas kernels: 61.9 us -> 56.1 us
    pallas_call x1, Pallas kernels: 61.9 us -> 56.1 us  [shards(): pl.pallas_call(kernel, out_shape=jax.ShapeDtypeStruct((ROWS, PER), BF16),...]
where the time goes in v2:
time: 57.9 us; the launch traced here: 57.8 us
  Pallas kernels  56.1 us (97%)
  local copies, waits for them, and re-layouts  1.67 us (3%)
    pallas_call x1, Pallas kernels, shards(): pl.pallas_call(kernel, out_shape=jax.ShapeDtypeStruct((ROWS, PER), BF16),...  56.1 us
    unnamed x1, local copies, waits for them, and re-layouts  1.67 us

profile of v2, /device:TPU:32, one launch (start us, length us, event | category | flops | bytes accessed | tf_op | source)
XLA Modules:
  0.0 57.8 jit_solution(11967717343054234684)
XLA Ops:
  0.0 56.1 %attend_project.1 = bf16[256,512]{1,0:T(8,128)(2,1)} custom-call(s32[32]{0:T(128)} %span_ref.1, s32[32,128]{1,0:T(8,128)} %bitcast.1, bf16[256,512]{1,0:T(8,128)(2,1)} %q_hbm.1, bf16[256,1024]{1,0:T(8,128)(2,1)} %k_hbm.1, bf16[256,1024]{1,0:T(8,128)(2,1)} %v_hbm.1, bf16[512,8192]{1,0:T(8,128)(2,1)} %w_hbm.1), custom_call_target="tpu_custom_call" | custom-call | tf_op jit(solution)/shard_map/attend_project/pallas_call | solution.py:284
  56.1 1.7 %copy.8 = bf16[256,512]{1,0:T(8,128)(2,1)} copy(bf16[256,512]{1,0:T(8,128)(2,1)} %attend_project.1) | data formatting | bytes 524288
